TPU v7x, 32 devices: a whole 2x2x4 slice. The times are simulated.
32 devices in a mesh: shard: 4 (over y, x), rep: 8 (over z, core).
Axes of the slice: x: 2, y: 2, z: 4, core: 2. Of those that a mesh axis runs over, the one named last changes fastest.
Arguments:
- activations: bfloat16 [8, 512, 2048], P('rep', 'shard'), may hold values from -16 to 16
- segments: int32 [8, 512], P('rep'), may hold values from 0 to 3, never falling along the last dimension, each value on 1 to 256 neighbouring positions
- attn_gain: float32 [2048], replicated, may hold values from 0.25 to 1.75
- query_weight: bfloat16 [2048, 2048], P('shard'), may hold values from -0.125 to 0.125
- key_weight: bfloat16 [2048, 1024], P('shard'), may hold values from -0.125 to 0.125
- value_weight: bfloat16 [2048, 1024], P('shard'), may hold values from -0.125 to 0.125
- query_gain: float32 [128], replicated, may hold values from 0.5 to 5.5
- key_gain: float32 [128], replicated, may hold values from 0.5 to 5.5
- out_weight: bfloat16 [2048, 2048], P('shard'), may hold values from -0.75 to 0.75
- mlp_gain: float32 [2048], replicated, may hold values from 0.25 to 1.75
- gate_weight: bfloat16 [2048, 6144], P('shard'), may hold values from -0.125 to 0.125
- up_weight: bfloat16 [2048, 6144], P('shard'), may hold values from -0.125 to 0.125
- down_weight: bfloat16 [6144, 2048], P('shard'), may hold values from -0.078125 to 0.078125
- cotangent: bfloat16 [8, 512, 2048], P('rep', 'shard'), may hold values from -11.1 to 11.1
Outputs:
- output: bfloat16 [8, 512, 2048], P('rep', 'shard')
- grad_input: float32 [8, 512, 2048], P('rep', 'shard')
- grad_attn_gain: float32 [2048], replicated
- grad_query_weight: float32 [2048, 2048], P('shard')
- grad_key_weight: float32 [2048, 1024], P('shard')
- grad_value_weight: float32 [2048, 1024], P('shard')
- grad_query_gain: float32 [128], replicated
- grad_key_gain: float32 [128], replicated
- grad_out_weight: float32 [2048, 2048], P('shard')
- grad_mlp_gain: float32 [2048], replicated
- grad_gate_weight: float32 [2048, 6144], P('shard')
- grad_up_weight: float32 [2048, 6144], P('shard')
- grad_down_weight: float32 [6144, 2048], P('shard')
Inputs may be any that keep to these rules, and one draw needn't show every extreme that they name: `segments`: within each sequence the document numbers never fall; each document has 1 to 256 tokens, and one has exactly 256.
All inputs are finite; a program needn't handle non-finite values.
Results may differ from a plain program's by a relative error of at most 0.02.
The roundings to bfloat16 on the way count: a program that leaves them out, or rounds other values in their place, can miss the bound.
Values may be sent and summed in bfloat16 or wider, within the bound.
A program may use at most 384 MiB of HBM per device.

v0:
```python
from functools import partial
import math
import jax
import jax.numpy as jnp
from jax import lax
from jax.sharding import PartitionSpec as P

HQ = 16
HK = 8
HD = 128
FF = 6144
EPSILON = 1e-06
ROPE_BASE = 1000000.0
MASKED = -1e30


def dims_last(left_op, right_op):
    return lax.dot_general(
        left_op, right_op, (((1,), (1,)), ((), ())), preferred_element_type=jnp.float32
    )


def dims_first(left_op, right_op):
    return lax.dot_general(
        left_op, right_op, (((0,), (0,)), ((), ())), preferred_element_type=jnp.float32
    )


def positions(seg_ids):
    token_index = jnp.arange(seg_ids.shape[0], dtype=jnp.int32)
    before = jnp.concatenate([jnp.full((1,), -1, jnp.int32), seg_ids[:-1]])
    starts = lax.cummax(
        jnp.where(seg_ids != before, token_index, jnp.zeros_like(token_index)), axis=0
    )
    return (token_index - starts).astype(jnp.float32)


def rotary(pos_float):
    half_width = HD // 2
    inv_freq = 1.0 / ROPE_BASE ** (jnp.arange(half_width, dtype=jnp.float32) * (2.0 / HD))
    angles = pos_float[:, None] * inv_freq[None, :]
    return (jnp.cos(angles), jnp.sin(angles))


def rotate(values_in, cosine, sine_part):
    half_width = values_in.shape[-1] // 2
    first_half = values_in[..., :half_width]
    second_half = values_in[..., half_width:]
    cos_b = cosine[:, None, :]
    sin_b = sine_part[:, None, :]
    return jnp.concatenate(
        [first_half * cos_b - second_half * sin_b, second_half * cos_b + first_half * sin_b], -1
    )


def rotate_back(grads_in, cosine, sine_part):
    half_width = grads_in.shape[-1] // 2
    first_half = grads_in[..., :half_width]
    second_half = grads_in[..., half_width:]
    cos_b = cosine[:, None, :]
    sin_b = sine_part[:, None, :]
    return jnp.concatenate(
        [first_half * cos_b + second_half * sin_b, second_half * cos_b - first_half * sin_b], -1
    )


def norm_back(grad_normed, values_in, rstat, gain_vec):
    scaled = values_in * rstat
    lead_axes = tuple(range(grad_normed.ndim - 1))
    grad_gain = jnp.sum(grad_normed * scaled, axis=lead_axes)
    weighted = grad_normed * gain_vec
    grad_values = rstat * (weighted - scaled * jnp.mean(weighted * scaled, -1, keepdims=True))
    return (grad_values, grad_gain)


def head_scores(query_group, key_block, visible, score_scale):
    scores = (
        jnp.einsum("qgd,kd->gqk", query_group, key_block, preferred_element_type=jnp.float32)
        * score_scale
    )
    return jnp.where(visible[None], scores, MASKED)


def attend(head_item, visible, score_scale):
    query_group, key_block, value_block = head_item
    scores = head_scores(query_group, key_block, visible, score_scale)
    row_max = jnp.max(scores, -1, keepdims=True)
    exp_scores = jnp.exp(scores - row_max)
    row_total = jnp.sum(exp_scores, -1, keepdims=True)
    softmax_out = (exp_scores / row_total).astype(jnp.bfloat16)
    head_out = jnp.einsum(
        "gqk,kd->qgd", softmax_out, value_block, preferred_element_type=jnp.float32
    )
    return (head_out, row_max + jnp.log(row_total))


def attend_back(head_item, visible, score_scale):
    query_group, key_block, value_block, grad_head, log_total = head_item
    scores = head_scores(query_group, key_block, visible, score_scale)
    softmax_out = jnp.exp(scores - log_total)
    grad_soft = jnp.einsum(
        "qgd,kd->gqk", grad_head, value_block, preferred_element_type=jnp.float32
    )
    row_delta = jnp.sum(softmax_out * grad_soft, -1, keepdims=True)
    grad_scores = (softmax_out * (grad_soft - row_delta)).astype(jnp.bfloat16)
    grad_group = (
        jnp.einsum("gqk,kd->qgd", grad_scores, key_block, preferred_element_type=jnp.float32)
        * score_scale
    )
    grad_key = (
        jnp.einsum("gqk,qgd->kd", grad_scores, query_group, preferred_element_type=jnp.float32)
        * score_scale
    )
    grad_value = jnp.einsum(
        "gqk,qgd->kd",
        softmax_out.astype(jnp.bfloat16),
        grad_head,
        preferred_element_type=jnp.float32,
    )
    return (grad_group, grad_key, grad_value)


def per_device(
    activations,
    segments,
    attn_gain,
    query_weight,
    key_weight,
    value_weight,
    query_gain,
    key_gain,
    out_weight,
    mlp_gain,
    gate_weight,
    up_weight,
    down_weight,
    cotangent,
):
    tok_rows = activations.shape[1]
    length = segments.shape[1]
    groups = HQ // HK
    score_scale = 1.0 / math.sqrt(HD)
    offset = lax.axis_index("shard") * tok_rows
    seg_ids = segments[0]
    pos_float = lax.dynamic_slice_in_dim(positions(seg_ids), offset, tok_rows)
    cosine, sine_part = rotary(pos_float)
    key_index = jnp.arange(length, dtype=jnp.int32)
    query_rows = offset + jnp.arange(tok_rows, dtype=jnp.int32)
    seg_rows = lax.dynamic_slice_in_dim(seg_ids, offset, tok_rows)
    visible = (key_index[None, :] <= query_rows[:, None]) & (seg_ids[None, :] == seg_rows[:, None])
    inputs = activations[0].astype(jnp.float32)
    rstat_attn = lax.rsqrt(jnp.mean(inputs * inputs, -1, keepdims=True) + EPSILON)
    normed = (inputs * rstat_attn * attn_gain).astype(jnp.bfloat16)
    full_query, full_key, full_value, full_out = (
        lax.all_gather(query_weight, "shard", axis=0, tiled=True),
        lax.all_gather(key_weight, "shard", axis=0, tiled=True),
        lax.all_gather(value_weight, "shard", axis=0, tiled=True),
        lax.all_gather(out_weight, "shard", axis=0, tiled=True),
    )
    queries = jnp.dot(normed, full_query, preferred_element_type=jnp.float32).reshape(
        tok_rows, HQ, HD
    )
    keys_raw = jnp.dot(normed, full_key, preferred_element_type=jnp.float32).reshape(
        tok_rows, HK, HD
    )
    values_low = jnp.dot(normed, full_value, preferred_element_type=jnp.float32).astype(
        jnp.bfloat16
    )
    query_rstat = lax.rsqrt(jnp.mean(queries * queries, -1, keepdims=True) + EPSILON)
    key_rstat = lax.rsqrt(jnp.mean(keys_raw * keys_raw, -1, keepdims=True) + EPSILON)
    query_rot = rotate(queries * query_rstat * query_gain, cosine, sine_part).astype(jnp.bfloat16)
    key_rot = rotate(keys_raw * key_rstat * key_gain, cosine, sine_part).astype(jnp.bfloat16)
    key_heads = jnp.transpose(key_rot, (1, 0, 2))
    value_heads = jnp.transpose(values_low.reshape(tok_rows, HK, HD), (1, 0, 2))
    all_keys, all_values = (
        lax.all_gather(key_heads, "shard", axis=1, tiled=True),
        lax.all_gather(value_heads, "shard", axis=1, tiled=True),
    )
    query_heads = jnp.transpose(query_rot.reshape(tok_rows, HK, groups, HD), (1, 0, 2, 3))
    attn_heads, log_totals = lax.map(
        partial(attend, visible=visible, score_scale=score_scale),
        (query_heads, all_keys, all_values),
    )
    attn_out = (
        jnp.transpose(attn_heads, (1, 0, 2, 3)).reshape(tok_rows, HQ * HD).astype(jnp.bfloat16)
    )
    hidden = inputs + jnp.dot(attn_out, full_out, preferred_element_type=jnp.float32)
    rstat_mlp = lax.rsqrt(jnp.mean(hidden * hidden, -1, keepdims=True) + EPSILON)
    normed_mlp = (hidden * rstat_mlp * mlp_gain).astype(jnp.bfloat16)
    full_gate, full_up, full_down = (
        lax.all_gather(gate_weight, "shard", axis=0, tiled=True),
        lax.all_gather(up_weight, "shard", axis=0, tiled=True),
        lax.all_gather(down_weight, "shard", axis=0, tiled=True),
    )
    gate_pre = jnp.dot(normed_mlp, full_gate, preferred_element_type=jnp.float32)
    up_pre = jnp.dot(normed_mlp, full_up, preferred_element_type=jnp.float32)
    sigmoid_gate = jax.nn.sigmoid(gate_pre)
    activated = (gate_pre * sigmoid_gate * up_pre).astype(jnp.bfloat16)
    result = hidden + jnp.dot(activated, full_down, preferred_element_type=jnp.float32)
    output = result.astype(jnp.bfloat16)[None]
    grad_out = cotangent[0]
    back_gate, back_up, back_down = (
        lax.all_gather(gate_weight, "shard", axis=0, tiled=True),
        lax.all_gather(up_weight, "shard", axis=0, tiled=True),
        lax.all_gather(down_weight, "shard", axis=0, tiled=True),
    )
    grad_act = dims_last(grad_out, back_down)
    grad_gate = (grad_act * up_pre * sigmoid_gate * (1.0 + gate_pre * (1.0 - sigmoid_gate))).astype(
        jnp.bfloat16
    )
    grad_up = (grad_act * gate_pre * sigmoid_gate).astype(jnp.bfloat16)
    grad_normed_mlp = dims_last(grad_gate, back_gate) + dims_last(grad_up, back_up)
    grad_hidden_part, grad_mlp_gain = norm_back(grad_normed_mlp, hidden, rstat_mlp, mlp_gain)
    grad_hidden = grad_out.astype(jnp.float32) + grad_hidden_part
    grad_branch = grad_hidden.astype(jnp.bfloat16)
    back_query, back_key, back_value, back_out = (
        lax.all_gather(query_weight, "shard", axis=0, tiled=True),
        lax.all_gather(key_weight, "shard", axis=0, tiled=True),
        lax.all_gather(value_weight, "shard", axis=0, tiled=True),
        lax.all_gather(out_weight, "shard", axis=0, tiled=True),
    )
    grad_attn = dims_last(grad_branch, back_out).astype(jnp.bfloat16)
    grad_heads = jnp.transpose(grad_attn.reshape(tok_rows, HK, groups, HD), (1, 0, 2, 3))
    grad_query_heads, grad_keys_all, grad_values_all = lax.map(
        partial(attend_back, visible=visible, score_scale=score_scale),
        (query_heads, all_keys, all_values, grad_heads, log_totals),
    )
    own_keys, own_values = (
        lax.psum_scatter(
            grad_keys_all.astype(jnp.bfloat16), "shard", scatter_dimension=1, tiled=True
        ).astype(jnp.float32),
        lax.psum_scatter(
            grad_values_all.astype(jnp.bfloat16), "shard", scatter_dimension=1, tiled=True
        ).astype(jnp.float32),
    )
    grad_query_rot = jnp.transpose(grad_query_heads, (1, 0, 2, 3)).reshape(tok_rows, HQ, HD)
    grad_key_rot = jnp.transpose(own_keys, (1, 0, 2))
    grad_value = (
        jnp.transpose(own_values, (1, 0, 2)).reshape(tok_rows, HK * HD).astype(jnp.bfloat16)
    )
    grad_query_norm, grad_query_gain = norm_back(
        rotate_back(grad_query_rot, cosine, sine_part), queries, query_rstat, query_gain
    )
    grad_key_norm, grad_key_gain = norm_back(
        rotate_back(grad_key_rot, cosine, sine_part), keys_raw, key_rstat, key_gain
    )
    grad_query = grad_query_norm.reshape(tok_rows, HQ * HD).astype(jnp.bfloat16)
    grad_key = grad_key_norm.reshape(tok_rows, HK * HD).astype(jnp.bfloat16)
    grad_normed = (
        dims_last(grad_query, back_query)
        + dims_last(grad_key, back_key)
        + dims_last(grad_value, back_value)
    )
    grad_input_part, grad_attn_gain = norm_back(grad_normed, inputs, rstat_attn, attn_gain)
    grad_input = (grad_hidden + grad_input_part)[None]
    grad_attn_gain, grad_query_gain, grad_key_gain, grad_mlp_gain = lax.psum(
        (grad_attn_gain, grad_query_gain, grad_key_gain, grad_mlp_gain), ("shard", "rep")
    )
    grad_qkv = jnp.concatenate([grad_query, grad_key, grad_value], 1)
    grad_mlp = jnp.concatenate([grad_gate, grad_up], 1)
    cols_attn, cols_mlp, cols_heads, cols_act = (
        lax.all_to_all(normed, "shard", split_axis=1, concat_axis=0, tiled=True),
        lax.all_to_all(normed_mlp, "shard", split_axis=1, concat_axis=0, tiled=True),
        lax.all_to_all(attn_out, "shard", split_axis=1, concat_axis=0, tiled=True),
        lax.all_to_all(activated, "shard", split_axis=1, concat_axis=0, tiled=True),
    )
    piece_qkv = lax.all_gather(grad_qkv, "shard", axis=0, tiled=True)
    piece_mlp = lax.all_gather(grad_mlp, "shard", axis=0, tiled=True)
    piece_branch = lax.all_gather(grad_branch, "shard", axis=0, tiled=True)
    piece_out = lax.all_gather(grad_out, "shard", axis=0, tiled=True)
    added_in = jnp.concatenate(
        [dims_first(cols_attn, piece_qkv), dims_first(cols_mlp, piece_mlp)], 1
    )
    part_out = dims_first(cols_heads, piece_branch)
    part_down = dims_first(cols_act, piece_out)
    owned_in, owned_out, owned_down = (
        lax.psum(added_in.astype(jnp.bfloat16), "rep").astype(jnp.float32),
        lax.psum(part_out.astype(jnp.bfloat16), "rep").astype(jnp.float32),
        lax.psum(part_down.astype(jnp.bfloat16), "rep").astype(jnp.float32),
    )
    width_query = HQ * HD
    width_kv = HK * HD
    edge_key = width_query + width_kv
    edge_value = edge_key + width_kv
    edge_gate = edge_value + FF
    grad_query_weight = owned_in[:, :width_query]
    grad_key_weight = owned_in[:, width_query:edge_key]
    grad_value_weight = owned_in[:, edge_key:edge_value]
    grad_gate_weight = owned_in[:, edge_value:edge_gate]
    grad_up_weight = owned_in[:, edge_gate:]
    return (
        output,
        grad_input,
        grad_attn_gain,
        grad_query_weight,
        grad_key_weight,
        grad_value_weight,
        grad_query_gain,
        grad_key_gain,
        owned_out,
        grad_mlp_gain,
        grad_gate_weight,
        grad_up_weight,
        owned_down,
    )


def solution(mesh):
    placed = (
        P("rep", "shard", None),
        P("rep", None),
        P(),
        P("shard", None),
        P("shard", None),
        P("shard", None),
        P(),
        P(),
        P("shard", None),
        P(),
        P("shard", None),
        P("shard", None),
        P("shard", None),
        P("rep", "shard", None),
    )
    return jax.shard_map(
        per_device,
        mesh=mesh,
        in_specs=placed,
        out_specs=(
            P("rep", "shard", None),
            P("rep", "shard", None),
            P(),
            P("shard", None),
            P("shard", None),
            P("shard", None),
            P(),
            P(),
            P("shard", None),
            P(),
            P("shard", None),
            P("shard", None),
            P("shard", None),
        ),
        check_vma=False,
    )
```

profile of v0, /device:TPU:0, one launch (start us, length us, event | category | flops | bytes accessed | tf_op | source)
XLA Modules:
  0.0 2083.6 jit_solution(7904533563809124515)
XLA Ops:
  11.7 53.4 %all-gather.19.cloned.1.call-done = bf16[2048,1024]{1,0:T(8,128)(2,1)} async-done(((bf16[512,1024]{1,0:T(8,128)(2,1)}), bf16[2048,1024]{1,0:T(8,128)(2,1)}) %all-gather.19.cloned.1.call-update) | async-done | bytes 4194320 | tf_op jit(solution)/shard_map/all_gather | solution.py:156
  65.2 6.5 copy.79
  71.7 3.7 multiply_reduce_fusion.9
  77.7 41.9 %all-gather.15.cloned.1.call-done = bf16[2048,1024]{1,0:T(8,128)(2,1)} async-done(((bf16[512,1024]{1,0:T(8,128)(2,1)}), bf16[2048,1024]{1,0:T(8,128)(2,1)}) %all-gather.15.cloned.1.call-update) | async-done | bytes 4194320 | tf_op jit(solution)/shard_map/all_gather | solution.py:157
  119.6 3.0 fusion.53
  128.3 20.1 all-gather.21.cloned.1.call-done
  150.0 87.6 %all-gather.23.cloned.1.call-done = bf16[2048,2048]{1,0:T(8,128)(2,1)} async-done(((bf16[512,2048]{1,0:T(8,128)(2,1)}), bf16[2048,2048]{1,0:T(8,128)(2,1)}) %all-gather.23.cloned.1.call-update) | async-done | bytes 8388624 | tf_op jit(solution)/shard_map/all_gather | solution.py:155
  237.6 12.2 copy.80
  249.9 5.8 multiply_reduce_fusion.6
  259.7 6.7 all-gather.17.cloned.1.call-done
  266.4 28.7 %while.30 = (s32[]{:T(128)}, bf16[8,128,2,128]{1,3,2,0:T(8,128)(2,1)}, f32[8,2,128,1]{2,1,3,0:T(2,128)}, bf16[8,512,128]{2,1,0:T(8,128)(2,1)}, bf16[8,512,128]{2...) while((s32[]{:T(128)}, ...), condition=%wide.region_8.9_spmd.clone.clone, body=%wide.region_5.8_spmd.clone.sunk.clone | while | flops 68353792 | bytes 2176605 | solution.py:180
  295.1 60.5 %all-gather.25.cloned.1.call-done = bf16[2048,2048]{1,0:T(8,128)(2,1)} async-done(((bf16[512,2048]{1,0:T(8,128)(2,1)}), bf16[2048,2048]{1,0:T(8,128)(2,1)}) %all-gather.25.cloned.1.call-update) | async-done | bytes 8388624 | tf_op jit(solution)/shard_map/all_gather | solution.py:158
  355.6 4.9 multiply_reduce_fusion.5
  360.8 224.3 %all-gather.27.cloned.1.call-done = bf16[2048,6144]{1,0:T(8,128)(2,1)} async-done(((bf16[512,6144]{1,0:T(8,128)(2,1)}), bf16[2048,6144]{1,0:T(8,128)(2,1)}) %all-gather.27.cloned.1.call-update) | async-done | bytes 25165840 | tf_op jit(solution)/shard_map/all_gather | solution.py:191
  585.1 13.7 fusion.86
  598.8 215.8 %all-gather.29.cloned.1.call-done = bf16[2048,6144]{1,0:T(8,128)(2,1)} async-done(((bf16[512,6144]{1,0:T(8,128)(2,1)}), bf16[2048,6144]{1,0:T(8,128)(2,1)}) %all-gather.29.cloned.1.call-update) | async-done | bytes 25165840 | tf_op jit(solution)/shard_map/all_gather | solution.py:192
  814.6 13.7 fusion.87
  828.3 215.8 %all-gather.31.cloned.1.call-done = bf16[6144,2048]{1,0:T(8,128)(2,1)} async-done(((bf16[1536,2048]{1,0:T(8,128)(2,1)}), bf16[6144,2048]{1,0:T(8,128)(2,1)}) %all-gather.31.cloned.1.call-update) | async-done | bytes 25165840 | tf_op jit(solution)/shard_map/all_gather | solution.py:193
  1044.1 16.8 multiply_convert_fusion.1
  1060.9 14.5 fusion.88
  1075.4 15.3 multiply_reduce_fusion.1
  1093.1 6.4 convolution_convert_fusion.4
  1102.7 86.9 %while.31 = (s32[]{:T(128)}, f32[8,128,2,128]{1,3,2,0:T(8,128)}, bf16[8,512,128]{1,2,0:T(8,128)(2,1)}, bf16[8,512,128]{1,2,0:T(8,128)(2,1)}, bf16[8,512,128]{2,1...) while((s32[]{:T(128)}, f32[8,128,2,128]{1,3,2,0:T(8,128)}, ...), condition=%wide.region_13.14_spmd.clone.clone, body=%wide.region_11.13_spmd.clone.sunk.clone | while | flops 169312000 | bytes 5780601 | solution.py:224
  1204.2 18.4 reduce-scatter.7.cloned.1.call-done
  1223.8 30.2 %reduce-scatter.9.cloned.1.call-done = bf16[128,1024]{1,0:T(8,128)(2,1)} async-done(((bf16[512,1024]{1,0:T(8,128)(2,1)}), bf16[128,1024]{1,0:T(8,128)(2,1)}) %reduce-scatter.9.cloned.1.call-update) | async-done | bytes 262160
  1256.8 3.8 pad_maximum_fusion.1
  1260.7 4.2 all-to-all-start.2
  1264.9 2.7 copy.136
  1267.6 9.6 all-to-all-done.2
  1277.3 4.4 all-to-all-start.3
  1288.6 23.6 %all-to-all-done.3 = bf16[128,4,1536]{2,0,1:T(8,128)(2,1)} async-done(((bf16[128,4,1536]{2,0,1:T(8,128)(2,1)}), bf16[128,4,1536]{2,0,1:T(8,128)(2,1)}, u32[]{:S(2)}, u32[]{:S(2)}) %all-to-all-start.3) | async-done | bytes 1572896 | tf_op jit(solution)/shard_map/all_to_all | solution.py:265
  1312.3 3.5 all-to-all-start
  1315.8 8.2 convolution_convert_fusion.1
  1324.0 25.4 %all-gather.37.cloned.1.call-done = bf16[512,2048]{1,0:T(8,128)(2,1)} async-done(((bf16[128,2048]{1,0:T(8,128)(2,1)}), bf16[512,2048]{1,0:T(8,128)(2,1)}) %all-gather.37.cloned.1.call-update) | async-done | bytes 2097168 | tf_op jit(solution)/shard_map/all_gather | solution.py:269
  1349.5 4.4 convolution_convert_fusion.3
  1354.6 3.5 all-to-all-start.1
  1358.2 49.5 %all-gather.33.cloned.1.call-done = bf16[512,4096]{0,1:T(8,128)(2,1)} async-done(((bf16[128,4096]{0,1:T(8,128)(2,1)}), bf16[512,4096]{0,1:T(8,128)(2,1)}) %all-gather.33.cloned.1.call-update) | async-done | bytes 4194320 | tf_op jit(solution)/shard_map/all_gather | solution.py:267
  1407.7 6.8 convolution_convert_fusion.2
  1414.5 117.9 %all-gather.35.cloned.1.call-done = bf16[512,12288]{1,0:T(8,128)(2,1)} async-done(((bf16[128,12288]{1,0:T(8,128)(2,1)}), bf16[512,12288]{1,0:T(8,128)(2,1)}) %all-gather.35.cloned.1.call-update) | async-done | bytes 12582928 | tf_op jit(solution)/shard_map/all_gather | solution.py:268
  1532.4 11.7 convolution_convert_fusion
  1544.1 9.0 pad_maximum_fusion
  1553.2 6.4 fusion.89
  1559.6 11.3 fusion.51
  1575.8 41.9 %all-reduce = (f32[2048]{0:T(1024)}, f32[128]{0:T(128)}, f32[128]{0:T(128)}, f32[2048]{0:T(1024)}) all-reduce(f32[2048]{0:T(1024)S(1)} %get-tuple-element.250, f32[128]{0:T(128)S(1)} %get-tuple-element.246, f32[128]{0:T(128)S(1)} %get-tuple-element.252, f32[2048]{0:T(1024)S(1)} %copy-done.29), channel_id=1, replica_groups=mesh['shard'=4,'rep'=8] {'shard','rep'}, use_global_device_ids=true, to_apply=%region_20.21 | all-reduce | flops 4352 | bytes 34816 | tf_op jit(solution)/shard_map/psum | solution.py:256
  1617.8 2.8 fusion.66
  1620.5 424.3 %all-reduce.4.cloned.1.call-done = (bf16[512,16384]{1,0:T(8,128)(2,1)}, bf16[512,2048]{1,0:T(8,128)(2,1)}, bf16[1536,2048]{1,0:T(8,128)(2,1)}) async-done(((bf16[512,16384]{1,0:T(8,128)(2,1)}, bf16[512,2048]{1,0:T(8,128)(2,1)}, bf16[1536,2048]{1,0:T(8,128)(2,1)}), (bf16[512,16384]{1,0:T(8,128)(2,1)}, bf16[512,2048]{1,0:T(8,128)(2,1)}, bf16[1536,2048]{1,0:T(8,128)(2,1)})) %all-reduce.4.cloned.1.call-update) | async-done | bytes 25165840 | tf_op jit(solution)/shard_map/psum | solution.py:277
  2044.9 15.6 fusion.84
  2068.0 6.3 convert_element_type.162
  (305 shorter events, 180.1 us)
Async XLA Ops:
  7.2 58.0 %all-gather.19.cloned.1.call-start = ((), (), s32[]{:S(2)}) async-start(), calls=%async_computation.8 | async-start | bytes 5242880 | tf_op jit(solution)/shard_map/all_gather | solution.py:156
  7.9 111.7 %all-gather.15.cloned.1.call-start = ((), (), s32[]{:S(2)}) async-start(), calls=%async_computation.6 | async-start | bytes 5242880 | tf_op jit(solution)/shard_map/all_gather | solution.py:157
  8.7 139.7 %all-gather.21.cloned.1.call-start = ((), (), s32[]{:S(2)}) async-start(), calls=%async_computation.9 | async-start | bytes 1310720 | tf_op jit(solution)/shard_map/all_gather | solution.py:176
  11.5 238.4 %copy-start.30 = (f32[128]{0:T(128)}, f32[128]{0:T(128)S(1)}, u32[]{:S(2)}) copy-start(f32[128]{0:T(128)S(1)} %add_rsqrt_fusion.3) | copy-start | bytes 1540
  11.7 244.3 %copy-start.18 = (f32[128,64]{0,1:T(8,128)}, f32[128,64]{0,1:T(8,128)S(1)}, u32[]{:S(2)}) copy-start(f32[128,64]{0,1:T(8,128)S(1)} %get-tuple-element.322) | copy-start | bytes 98308
  11.7 244.3 %copy-start.20 = (f32[128,64]{0,1:T(8,128)}, f32[128,64]{0,1:T(8,128)S(1)}, u32[]{:S(2)}) copy-start(f32[128,64]{0,1:T(8,128)S(1)} %get-tuple-element.323) | copy-start | bytes 98308
  65.2 6.5 copy-start.1
  65.2 6.5 copy-start.24
  77.1 160.5 %all-gather.23.cloned.1.call-start = ((), (), s32[]{:S(2)}) async-start(), calls=%async_computation.10 | async-start | bytes 10485760 | tf_op jit(solution)/shard_map/all_gather | solution.py:155
  77.7 188.7 %all-gather.17.cloned.1.call-start = ((), (), s32[]{:S(2)}) async-start(), calls=%async_computation.7 | async-start | bytes 1310720 | tf_op jit(solution)/shard_map/all_gather | solution.py:177
  123.3 232.3 %all-gather.25.cloned.1.call-start = ((), (), s32[]{:S(2)}) async-start(), calls=%async_computation.11 | async-start | bytes 10485760 | tf_op jit(solution)/shard_map/all_gather | solution.py:158
  123.9 461.2 %all-gather.27.cloned.1.call-start = ((), (), s32[]{:S(2)}) async-start(), calls=%async_computation.12 | async-start | bytes 31457280 | tf_op jit(solution)/shard_map/all_gather | solution.py:191
  124.7 689.9 %all-gather.29.cloned.1.call-start = ((), (), s32[]{:S(2)}) async-start(), calls=%async_computation.13 | async-start | bytes 31457280 | tf_op jit(solution)/shard_map/all_gather | solution.py:192
  125.4 918.6 %all-gather.31.cloned.1.call-start = ((), (), s32[]{:S(2)}) async-start(), calls=%async_computation.14 | async-start | bytes 31457280 | tf_op jit(solution)/shard_map/all_gather | solution.py:193
  126.2 1096.4 %reduce-scatter.7.cloned.1.call-start = ((), (), s32[]{:S(2)}) async-start(), calls=%async_computation.19 | async-start | bytes 1310720
  255.7 10.7 copy-start.27
  295.1 60.5 %copy-start.7 = (bf16[8,512,128]{2,1,0:T(8,128)(2,1)}, bf16[8,512,128]{2,1,0:T(8,128)(2,1)S(1)}, u32[]{:S(2)}) copy-start(bf16[8,512,128]{2,1,0:T(8,128)(2,1)S(1)} %get-tuple-element.616) | copy-start | bytes 3145732
  295.1 60.5 %copy-start.14 = (bf16[8,128,2,128]{3,1,2,0:T(8,128)(2,1)}, bf16[8,128,2,128]{3,1,2,0:T(8,128)(2,1)S(1)}, u32[]{:S(2)}) copy-start(bf16[8,128,2,128]{3,1,2,0:T(8,128)(2,1)S(1)} %get-tuple-element.632) | copy-start | bytes 1572868
  360.6 730.1 %copy-start.32 = (f32[128]{0:T(128)}, f32[128]{0:T(128)S(1)}, u32[]{:S(2)}) copy-start(f32[128]{0:T(128)S(1)} %add_rsqrt_fusion.2) | copy-start | bytes 1540
  360.8 453.8 %copy-start.4 = (bf16[128,2048]{1,0:T(8,128)(2,1)}, bf16[128,2048]{1,0:T(8,128)(2,1)S(1)}, u32[]{:S(2)}) copy-start(bf16[128,2048]{1,0:T(8,128)(2,1)S(1)} %multiply_convert_fusion.5) | copy-start | bytes 1572868
  1075.4 15.3 copy-start.11
  1090.7 8.8 copy-start.38
  1194.5 6.8 copy-start.19
  1194.5 6.8 copy-start.21
  1194.5 59.5 %reduce-scatter.9.cloned.1.call-start = ((), (), s32[]{:S(2)}) async-start(), calls=%async_computation.20 | async-start | bytes 1310720
  1194.5 8.1 copy-start.28
  1194.5 8.1 copy-start.37
  1199.5 116.3 %all-gather.39.cloned.1.call-start = ((), (), s32[]{:S(2)}) async-start(), calls=%async_computation.18 | async-start | bytes 2621440 | tf_op jit(solution)/shard_map/all_gather | solution.py:270
  1200.1 149.4 %all-gather.37.cloned.1.call-start = ((), (), s32[]{:S(2)}) async-start(), calls=%async_computation.17 | async-start | bytes 2621440 | tf_op jit(solution)/shard_map/all_gather | solution.py:269
  1200.8 206.9 %all-gather.33.cloned.1.call-start = ((), (), s32[]{:S(2)}) async-start(), calls=%async_computation.15 | async-start | bytes 5242880 | tf_op jit(solution)/shard_map/all_gather | solution.py:267
  1202.7 52.7 %copy-start.9 = (f32[128,8,128]{0,2,1:T(8,128)S(1)}, f32[128,8,128]{0,2,1:T(8,128)}, u32[]{:S(2)}) copy-start(f32[128,8,128]{0,2,1:T(8,128)} %copy-done.8) | copy-start | bytes 1572868
  1202.7 52.7 %copy-start.35 = (f32[128]{0:T(128)S(1)}, f32[128]{0:T(128)}, u32[]{:S(2)}) copy-start(f32[128]{0:T(128)} %param.25) | copy-start | bytes 1540
  1204.2 51.5 %copy-start.13 = (bf16[128,16,128]{0,2,1:T(8,128)(2,1)S(1)}, bf16[128,16,128]{0,2,1:T(8,128)(2,1)}, u32[]{:S(2)}) copy-start(bf16[128,16,128]{0,2,1:T(8,128)(2,1)} %multiply_convert_fusion.4) | copy-start | bytes 1572868
  1256.8 275.6 %all-gather.35.cloned.1.call-start = ((), (), s32[]{:S(2)}) async-start(), calls=%async_computation.16 | async-start | bytes 15728640 | tf_op jit(solution)/shard_map/all_gather | solution.py:268
  1260.7 16.6 all-to-all-start.2
  1264.9 18.5 copy-start.31
  1264.9 20.9 %copy-start.5 = (bf16[128,2048]{1,0:T(8,128)(2,1)S(1)}, bf16[128,2048]{1,0:T(8,128)(2,1)}, u32[]{:S(2)}) copy-start(bf16[128,2048]{1,0:T(8,128)(2,1)} %copy-done.4) | copy-start | bytes 1572868
  1277.3 35.0 %all-to-all-start.3 = ((bf16[128,4,1536]{2,0,1:T(8,128)(2,1)}), bf16[128,4,1536]{2,0,1:T(8,128)(2,1)}, u32[]{:S(2)}, u32[]{:S(2)}) async-start(bf16[128,4,1536]{2,0,1:T(8,128)(2,1)} %bitcast.331), calls=%async_computation.3 | async-start | bytes 3145728 | tf_op jit(solution)/shard_map/all_to_all | solution.py:265
  1312.3 41.6 %all-to-all-start = ((bf16[128,4,512]{2,0,1:T(8,128)(2,1)}), bf16[128,4,512]{2,0,1:T(8,128)(2,1)S(1)}, u32[]{:S(2)}, u32[]{:S(2)}) async-start(bf16[128,4,512]{2,0,1:T(8,128)(2,1)} %fusion.56), calls=%async_computation | async-start | bytes 1048576 | tf_op jit(solution)/shard_map/all_to_all | solution.py:262
  1354.6 59.8 %all-to-all-start.1 = ((bf16[128,4,512]{2,0,1:T(8,128)(2,1)}), bf16[128,4,512]{2,0,1:T(8,128)(2,1)S(1)}, u32[]{:S(2)}, u32[]{:S(2)}) async-start(bf16[128,4,512]{2,0,1:T(8,128)(2,1)} %bitcast.345), calls=%async_computation.1 | async-start | bytes 1048576 | tf_op jit(solution)/shard_map/all_to_all | solution.py:263
  1358.1 686.8 %all-reduce.4.cloned.1.call-start = ((), (), s32[]{:S(2)}) async-start(), calls=%async_computation.21 | async-start | bytes 50331648 | tf_op jit(solution)/shard_map/psum | solution.py:277
  1559.6 11.3 copy-start.3
  1573.1 44.6 %copy-start.6 = (f32[128,2048]{1,0:T(8,128)S(1)}, f32[128,2048]{1,0:T(8,128)}, u32[]{:S(2)}) copy-start(f32[128,2048]{1,0:T(8,128)} %get-tuple-element.330) | copy-start | bytes 3145732
  1573.1 44.6 %copy-start.12 = (bf16[1,128,2048]{2,1,0:T(8,128)(2,1)S(1)}, bf16[1,128,2048]{2,1,0:T(8,128)(2,1)}, u32[]{:S(2)}) copy-start(bf16[1,128,2048]{2,1,0:T(8,128)(2,1)} %param.31) | copy-start | bytes 1572868
  1573.1 44.6 %copy-start.26 = (f32[2048]{0:T(1024)S(1)}, f32[2048]{0:T(1024)}, u32[]{:S(2)}) copy-start(f32[2048]{0:T(1024)} %param.27) | copy-start | bytes 24580
  1573.1 44.6 %copy-start.33 = (f32[128]{0:T(128)S(1)}, f32[128]{0:T(128)}, u32[]{:S(2)}) copy-start(f32[128]{0:T(128)} %copy-done.32) | copy-start | bytes 1540
  1573.1 44.6 %copy-start.39 = (f32[128]{0:T(128)S(1)}, f32[128]{0:T(128)}, u32[]{:S(2)}) copy-start(f32[128]{0:T(128)} %copy-done.38) | copy-start | bytes 1540
  2044.9 18.0 copy-start
  (14 other events, 50.9 us)
Sparse Core Ops, SparseCore 0:
  9.8 55.2 all-gather.18
  67.0 52.5 all-gather.14
  122.0 26.3 all-gather.20
  150.1 87.4 all-gather.22
  239.9 26.4 all-gather.16
  268.1 87.4 all-gather.24
  357.5 227.5 all-gather.26
  587.0 227.5 all-gather.28
  816.4 227.5 all-gather.30
  1194.6 27.9 reduce-scatter.6
  1226.0 27.9 reduce-scatter.8
  1255.7 56.7 all-gather.38
  1314.3 35.1 all-gather.36
  1351.7 55.9 all-gather.32
  1410.0 122.3 all-gather.34
  1553.3 491.5 all-reduce.3
where the time goes:
time: 2090 us; the launch traced here: 2080 us
  waiting for transfers between devices  1630 us (78%)
  matrix products  228 us (11%)
  local copies, waits for them, and re-layouts  91.2 us (4%)
  other arithmetic  59.5 us (3%)
  blocking collectives  41.9 us (2%)
    psum x1, waiting for transfers between devices, per_device(): lax.psum(added_in.astype(jnp.bfloat16), 'rep').astype(jnp.float32)  424 us
    all_gather x1, waiting for transfers between devices, per_device(): lax.all_gather(gate_weight, 'shard', axis=0, tiled=True)  224 us
    all_gather x1, waiting for transfers between devices, per_device(): lax.all_gather(down_weight, 'shard', axis=0, tiled=True)  216 us
    all_gather x1, waiting for transfers between devices, per_device(): lax.all_gather(up_weight, 'shard', axis=0, tiled=True)  216 us
    all_gather x1, waiting for transfers between devices, per_device(): piece_mlp = lax.all_gather(grad_mlp, 'shard', axis=0, tiled=True)  118 us
    all_gather x1, waiting for transfers between devices, per_device(): lax.all_gather(query_weight, 'shard', axis=0, tiled=True)  87.6 us
    dot_general x7, matrix products, dims_last(): lax.dot_general(left_op, right_op, (((1,), (1,)), ((), ())), preferred_el...  63.7 us
    all_gather x1, waiting for transfers between devices, per_device(): lax.all_gather(out_weight, 'shard', axis=0, tiled=True)  60.5 us
  transfers between devices with their start and end apart: 20, of which 17 were waited for; matrix products, arithmetic and copies ran while one was open for 8% of the time, Pallas kernels for 0%

commit v1 on v0

--- a/solution.py
+++ b/solution.py
@@ -274,7 +274,7 @@
     part_out = dims_first(cols_heads, piece_branch)
     part_down = dims_first(cols_act, piece_out)
     owned_in, owned_out, owned_down = (
-        lax.psum(added_in.astype(jnp.bfloat16), "rep").astype(jnp.float32),
+        jnp.sum(lax.all_gather(added_in.astype(jnp.bfloat16), "rep"), axis=0).astype(jnp.float32),
         lax.psum(part_out.astype(jnp.bfloat16), "rep").astype(jnp.float32),
         lax.psum(part_down.astype(jnp.bfloat16), "rep").astype(jnp.float32),
     )

time: 2090 us -> 2890 us (1.38)
  waiting for transfers between devices: 1630 us -> 2410 us
  other arithmetic: 59.5 us -> 100 us
    all_gather x0 -> x1, waiting for transfers between devices: none -> 1100 us  [per_device(): lax.all_gather(added_in.astype(jnp.bfloat16), 'rep')]
    psum x1, waiting for transfers between devices: 424 us -> 94.1 us  [per_device(): lax.psum(part_out.astype(jnp.bfloat16), 'rep').astype(jnp.float32)]
    reduce_sum x0 -> x1, other arithmetic: none -> 50 us  [per_device(): jnp.sum(lax.all_gather(added_in.astype(jnp.bfloat16), 'rep'), axis=0)]
  transfers between devices with their start and end apart: 20 -> 21, of which waited for: 17 -> 18; matrix products, arithmetic and copies ran while one was open for 8% -> 7% of each run, Pallas kernels for 0% -> 0%
where the time goes in v1:
time: 2890 us; the launch traced here: 2880 us
  waiting for transfers between devices  2410 us (83%)
  matrix products  227 us (8%)
  other arithmetic  100 us (3%)
  local copies, waits for them, and re-layouts  74 us (3%)
  blocking collectives  41.2 us (1%)
    all_gather x1, waiting for transfers between devices, per_device(): lax.all_gather(added_in.astype(jnp.bfloat16), 'rep')  1100 us
    all_gather x1, waiting for transfers between devices, per_device(): lax.all_gather(gate_weight, 'shard', axis=0, tiled=True)  224 us
    all_gather x1, waiting for transfers between devices, per_device(): lax.all_gather(down_weight, 'shard', axis=0, tiled=True)  216 us
    all_gather x1, waiting for transfers between devices, per_device(): lax.all_gather(up_weight, 'shard', axis=0, tiled=True)  216 us
    all_gather x1, waiting for transfers between devices, per_device(): piece_mlp = lax.all_gather(grad_mlp, 'shard', axis=0, tiled=True)  118 us
    psum x1, waiting for transfers between devices, per_device(): lax.psum(part_out.astype(jnp.bfloat16), 'rep').astype(jnp.float32)  94.1 us
    all_gather x1, waiting for transfers between devices, per_device(): lax.all_gather(query_weight, 'shard', axis=0, tiled=True)  87.6 us
    all_gather x1, waiting for transfers between devices, per_device(): lax.all_gather(out_weight, 'shard', axis=0, tiled=True)  63.7 us
  transfers between devices with their start and end apart: 21, of which 18 were waited for; matrix products, arithmetic and copies ran while one was open for 7% of the time, Pallas kernels for 0%

profile of v1, /device:TPU:0, one launch (start us, length us, event | category | flops | bytes accessed | tf_op | source)
XLA Modules:
  0.0 2881.1 jit_solution(2364602055634660010)
XLA Ops:
  11.7 53.5 %all-gather.20.cloned.1.call-done = bf16[2048,1024]{1,0:T(8,128)(2,1)} async-done(((bf16[512,1024]{1,0:T(8,128)(2,1)}), bf16[2048,1024]{1,0:T(8,128)(2,1)}) %all-gather.20.cloned.1.call-update) | async-done | bytes 4194320 | tf_op jit(solution)/shard_map/all_gather | solution.py:156
  65.2 6.5 copy.79
  77.7 41.9 %all-gather.16.cloned.1.call-done = bf16[2048,1024]{1,0:T(8,128)(2,1)} async-done(((bf16[512,1024]{1,0:T(8,128)(2,1)}), bf16[2048,1024]{1,0:T(8,128)(2,1)}) %all-gather.16.cloned.1.call-update) | async-done | bytes 4194320 | tf_op jit(solution)/shard_map/all_gather | solution.py:157
  127.2 21.2 all-gather.22.cloned.1.call-done
  150.0 87.6 %all-gather.24.cloned.1.call-done = bf16[2048,2048]{1,0:T(8,128)(2,1)} async-done(((bf16[512,2048]{1,0:T(8,128)(2,1)}), bf16[2048,2048]{1,0:T(8,128)(2,1)}) %all-gather.24.cloned.1.call-update) | async-done | bytes 8388624 | tf_op jit(solution)/shard_map/all_gather | solution.py:155
  237.6 12.2 copy.80
  249.9 5.8 multiply_reduce_fusion.6
  261.2 5.2 all-gather.18.cloned.1.call-done
  266.4 25.5 while.30
  292.0 63.7 %all-gather.26.cloned.1.call-done = bf16[2048,2048]{1,0:T(8,128)(2,1)} async-done(((bf16[512,2048]{1,0:T(8,128)(2,1)}), bf16[2048,2048]{1,0:T(8,128)(2,1)}) %all-gather.26.cloned.1.call-update) | async-done | bytes 8388624 | tf_op jit(solution)/shard_map/all_gather | solution.py:158
  355.7 4.9 multiply_reduce_fusion.5
  360.8 224.3 %all-gather.28.cloned.1.call-done = bf16[2048,6144]{1,0:T(8,128)(2,1)} async-done(((bf16[512,6144]{1,0:T(8,128)(2,1)}), bf16[2048,6144]{1,0:T(8,128)(2,1)}) %all-gather.28.cloned.1.call-update) | async-done | bytes 25165840 | tf_op jit(solution)/shard_map/all_gather | solution.py:191
  585.1 13.7 fusion.88
  598.8 215.8 %all-gather.30.cloned.1.call-done = bf16[2048,6144]{1,0:T(8,128)(2,1)} async-done(((bf16[512,6144]{1,0:T(8,128)(2,1)}), bf16[2048,6144]{1,0:T(8,128)(2,1)}) %all-gather.30.cloned.1.call-update) | async-done | bytes 25165840 | tf_op jit(solution)/shard_map/all_gather | solution.py:192
  814.6 13.7 fusion.89
  828.3 215.8 %all-gather.32.cloned.1.call-done = bf16[6144,2048]{1,0:T(8,128)(2,1)} async-done(((bf16[1536,2048]{1,0:T(8,128)(2,1)}), bf16[6144,2048]{1,0:T(8,128)(2,1)}) %all-gather.32.cloned.1.call-update) | async-done | bytes 25165840 | tf_op jit(solution)/shard_map/all_gather | solution.py:193
  1044.1 16.8 multiply_convert_fusion.1
  1060.9 14.7 fusion.90
  1075.6 14.7 multiply_reduce_fusion.1
  1092.7 6.4 convolution_convert_fusion.4
  1102.2 63.8 %while.31 = (s32[]{:T(128)}, f32[8,128,2,128]{1,3,2,0:T(8,128)}, bf16[8,512,128]{1,2,0:T(8,128)(2,1)}, bf16[8,512,128]{1,2,0:T(8,128)(2,1)}, bf16[8,512,128]{2,1...) while((s32[]{:T(128)}, f32[8,128,2,128]{1,3,2,0:T(8,128)}, ...), condition=%wide.region_13.14_spmd.clone.clone, body=%wide.region_11.13_spmd.clone.sunk.clone | while | flops 169312000 | bytes 5779593 | solution.py:224
  1180.3 18.7 reduce-scatter.7.cloned.1.call-done
  1200.9 29.5 %reduce-scatter.9.cloned.1.call-done = bf16[128,1024]{1,0:T(8,128)(2,1)} async-done(((bf16[512,1024]{1,0:T(8,128)(2,1)}), bf16[128,1024]{1,0:T(8,128)(2,1)}) %reduce-scatter.9.cloned.1.call-update) | async-done | bytes 262160
  1234.2 3.8 pad_maximum_fusion.1
  1238.0 4.2 all-to-all-start.2
  1245.0 8.9 all-to-all-done.2
  1253.8 4.3 all-to-all-start.3
  1265.2 23.5 all-to-all-done.3
  1292.3 8.2 convolution_convert_fusion.1
  1300.5 25.4 all-gather.40.cloned.1.call-done
  1326.0 4.4 convolution_convert_fusion.3
  1330.4 4.2 all-to-all-start.1
  1334.6 49.5 %all-gather.34.cloned.1.call-done = bf16[512,4096]{0,1:T(8,128)(2,1)} async-done(((bf16[128,4096]{0,1:T(8,128)(2,1)}), bf16[512,4096]{0,1:T(8,128)(2,1)}) %all-gather.34.cloned.1.call-update) | async-done | bytes 4194320 | tf_op jit(solution)/shard_map/all_gather | solution.py:267
  1384.1 6.6 fusion.51
  1390.7 118.1 %all-gather.36.cloned.1.call-done = bf16[512,12288]{1,0:T(8,128)(2,1)} async-done(((bf16[128,12288]{1,0:T(8,128)(2,1)}), bf16[512,12288]{1,0:T(8,128)(2,1)}) %all-gather.36.cloned.1.call-update) | async-done | bytes 12582928 | tf_op jit(solution)/shard_map/all_gather | solution.py:268
  1508.8 10.0 fusion.50
  1518.8 9.1 pad_maximum_fusion
  1527.9 6.5 fusion.91
  1534.4 11.3 fusion.53
  1550.7 41.2 %all-reduce = (f32[2048]{0:T(1024)}, f32[128]{0:T(128)}, f32[128]{0:T(128)}, f32[2048]{0:T(1024)}) all-reduce(f32[2048]{0:T(1024)S(1)} %get-tuple-element.250, f32[128]{0:T(128)S(1)} %get-tuple-element.246, f32[128]{0:T(128)S(1)} %get-tuple-element.252, ...), channel_id=1, replica_groups=mesh['shard'=4,'rep'=8] {'shard','rep'}, use_global_device_ids=true, to_apply=%region_20.21 | all-reduce | flops 4352 | bytes 34816 | tf_op jit(solution)/shard_map/psum | solution.py:256
  1594.8 94.1 %all-reduce.4.cloned.1.call-done = (bf16[512,2048]{1,0:T(8,128)(2,1)}, bf16[1536,2048]{1,0:T(8,128)(2,1)}) async-done(((bf16[512,2048]{1,0:T(8,128)(2,1)}, bf16[1536,2048]{1,0:T(8,128)(2,1)}), (bf16[512,2048]{1,0:T(8,128)(2,1)}, bf16[1536,2048]{1,0:T(8,128)(2,1)})) %all-reduce.4.cloned.1.call-update) | async-done | bytes 8388624 | tf_op jit(solution)/shard_map/psum | solution.py:278
  1688.8 4.3 convert_element_type.169
  1693.1 8.6 convert_element_type.171
  1701.7 1103.4 %all-gather.38.cloned.1.call-done = bf16[8,512,16384]{2,1,0:T(8,128)(2,1)} async-done(((bf16[1,512,16384]{2,1,0:T(8,128)(2,1)}), bf16[8,512,16384]{2,1,0:T(8,128)(2,1)}) %all-gather.38.cloned.1.call-update) | async-done | bytes 134217744 | tf_op jit(solution)/shard_map/all_gather | solution.py:277
  2805.1 50.0 %reduce_sum.147 = bf16[512,16384]{1,0:T(8,128)(2,1)} reduce(bf16[8,512,16384]{2,1,0:T(8,128)(2,1)} %all-gather.38.cloned.1.call-done, bf16[]{:T(256)} %constant.94.clone.1), dimensions={0}, to_apply=%region_21.22 | reduce | flops 58720256 | bytes 150994944 | tf_op jit(solution)/shard_map/reduce_sum | solution.py:277
  2855.2 4.4 slice.77
  2859.6 4.8 fusion.87
  2864.7 9.5 fusion.86
  (264 shorter events, 160.6 us)
Async XLA Ops:
  7.2 58.0 %all-gather.20.cloned.1.call-start = ((), (), s32[]{:S(2)}) async-start(), calls=%async_computation.8 | async-start | bytes 5242880 | tf_op jit(solution)/shard_map/all_gather | solution.py:156
  7.9 111.7 %all-gather.16.cloned.1.call-start = ((), (), s32[]{:S(2)}) async-start(), calls=%async_computation.6 | async-start | bytes 5242880 | tf_op jit(solution)/shard_map/all_gather | solution.py:157
  8.7 139.7 %all-gather.22.cloned.1.call-start = ((), (), s32[]{:S(2)}) async-start(), calls=%async_computation.9 | async-start | bytes 1310720 | tf_op jit(solution)/shard_map/all_gather | solution.py:176
  65.2 6.5 copy-start.1
  65.2 6.5 copy-start.16
  71.6 4.5 copy-start.18
  75.4 0.8 copy-start.8
  77.1 160.5 %all-gather.24.cloned.1.call-start = ((), (), s32[]{:S(2)}) async-start(), calls=%async_computation.10 | async-start | bytes 10485760 | tf_op jit(solution)/shard_map/all_gather | solution.py:155
  77.7 188.7 %all-gather.18.cloned.1.call-start = ((), (), s32[]{:S(2)}) async-start(), calls=%async_computation.7 | async-start | bytes 1310720 | tf_op jit(solution)/shard_map/all_gather | solution.py:177
  123.3 232.3 %all-gather.26.cloned.1.call-start = ((), (), s32[]{:S(2)}) async-start(), calls=%async_computation.11 | async-start | bytes 10485760 | tf_op jit(solution)/shard_map/all_gather | solution.py:158
  123.9 461.2 %all-gather.28.cloned.1.call-start = ((), (), s32[]{:S(2)}) async-start(), calls=%async_computation.12 | async-start | bytes 31457280 | tf_op jit(solution)/shard_map/all_gather | solution.py:191
  124.7 689.9 %all-gather.30.cloned.1.call-start = ((), (), s32[]{:S(2)}) async-start(), calls=%async_computation.13 | async-start | bytes 31457280 | tf_op jit(solution)/shard_map/all_gather | solution.py:192
  125.4 0.8 copy-start.15
  125.4 918.6 %all-gather.32.cloned.1.call-start = ((), (), s32[]{:S(2)}) async-start(), calls=%async_computation.14 | async-start | bytes 31457280 | tf_op jit(solution)/shard_map/all_gather | solution.py:193
  126.2 1072.8 %reduce-scatter.7.cloned.1.call-start = ((), (), s32[]{:S(2)}) async-start(), calls=%async_computation.20 | async-start | bytes 1310720
  249.9 5.8 copy-start.19
  291.9 63.7 %copy-start.7 = (bf16[8,512,128]{2,1,0:T(8,128)(2,1)}, bf16[8,512,128]{2,1,0:T(8,128)(2,1)S(1)}, u32[]{:S(2)}) copy-start(bf16[8,512,128]{2,1,0:T(8,128)(2,1)S(1)} %get-tuple-element.611) | copy-start | bytes 3145732
  355.6 5.0 copy-start.17
  360.8 453.8 %copy-start.4 = (bf16[128,2048]{1,0:T(8,128)(2,1)}, bf16[128,2048]{1,0:T(8,128)(2,1)S(1)}, u32[]{:S(2)}) copy-start(bf16[128,2048]{1,0:T(8,128)(2,1)S(1)} %multiply_convert_fusion.5) | copy-start | bytes 1572868
  1075.6 14.7 copy-start.12
  1170.9 59.5 %reduce-scatter.9.cloned.1.call-start = ((), (), s32[]{:S(2)}) async-start(), calls=%async_computation.21 | async-start | bytes 1310720
  1175.9 116.4 %all-gather.42.cloned.1.call-start = ((), (), s32[]{:S(2)}) async-start(), calls=%async_computation.19 | async-start | bytes 2621440 | tf_op jit(solution)/shard_map/all_gather | solution.py:270
  1176.5 149.5 %all-gather.40.cloned.1.call-start = ((), (), s32[]{:S(2)}) async-start(), calls=%async_computation.18 | async-start | bytes 2621440 | tf_op jit(solution)/shard_map/all_gather | solution.py:269
  1177.2 206.9 %all-gather.34.cloned.1.call-start = ((), (), s32[]{:S(2)}) async-start(), calls=%async_computation.15 | async-start | bytes 5242880 | tf_op jit(solution)/shard_map/all_gather | solution.py:267
  1178.8 53.9 %copy-start.9 = (f32[128,8,128]{0,2,1:T(8,128)S(1)}, f32[128,8,128]{0,2,1:T(8,128)}, u32[]{:S(2)}) copy-start(f32[128,8,128]{0,2,1:T(8,128)} %copy-done.8) | copy-start | bytes 1572868
  1180.3 52.7 %copy-start.14 = (bf16[128,16,128]{0,2,1:T(8,128)(2,1)S(1)}, bf16[128,16,128]{0,2,1:T(8,128)(2,1)}, u32[]{:S(2)}) copy-start(bf16[128,16,128]{0,2,1:T(8,128)(2,1)} %multiply_convert_fusion.4) | copy-start | bytes 1572868
  1234.1 274.6 %all-gather.36.cloned.1.call-start = ((), (), s32[]{:S(2)}) async-start(), calls=%async_computation.16 | async-start | bytes 15728640 | tf_op jit(solution)/shard_map/all_gather | solution.py:268
  1238.0 15.8 all-to-all-start.2
  1242.2 20.1 copy-start.5
  1253.8 34.9 %all-to-all-start.3 = ((bf16[128,4,1536]{2,0,1:T(8,128)(2,1)}), bf16[128,4,1536]{2,0,1:T(8,128)(2,1)}, u32[]{:S(2)}, u32[]{:S(2)}) async-start(bf16[128,4,1536]{2,0,1:T(8,128)(2,1)} %bitcast.335), calls=%async_computation.3 | async-start | bytes 3145728 | tf_op jit(solution)/shard_map/all_to_all | solution.py:265
  1288.7 41.6 %all-to-all-start = ((bf16[128,4,512]{2,0,1:T(8,128)(2,1)}), bf16[128,4,512]{2,0,1:T(8,128)(2,1)S(1)}, u32[]{:S(2)}, u32[]{:S(2)}) async-start(bf16[128,4,512]{2,0,1:T(8,128)(2,1)} %fusion.58), calls=%async_computation | async-start | bytes 1048576 | tf_op jit(solution)/shard_map/all_to_all | solution.py:262
  1292.2 396.6 %all-reduce.4.cloned.1.call-start = ((), (), s32[]{:S(2)}) async-start(), calls=%async_computation.22 | async-start | bytes 16777216 | tf_op jit(solution)/shard_map/psum | solution.py:278
  1330.4 60.4 %all-to-all-start.1 = ((bf16[128,4,512]{2,0,1:T(8,128)(2,1)}), bf16[128,4,512]{2,0,1:T(8,128)(2,1)}, u32[]{:S(2)}, u32[]{:S(2)}) async-start(bf16[128,4,512]{2,0,1:T(8,128)(2,1)} %bitcast.264), calls=%async_computation.1 | async-start | bytes 1048576 | tf_op jit(solution)/shard_map/all_to_all | solution.py:263
  1334.5 1470.6 %all-gather.38.cloned.1.call-start = ((), (), s32[]{:S(2)}) async-start(), calls=%async_computation.17 | async-start | bytes 150994944 | tf_op jit(solution)/shard_map/all_gather | solution.py:277
  1527.9 6.5 copy-start.10
  1534.4 11.3 copy-start.3
  1545.7 2.3 copy-start.2
  1548.0 43.9 %copy-start.6 = (f32[128,2048]{1,0:T(8,128)S(1)}, f32[128,2048]{1,0:T(8,128)}, u32[]{:S(2)}) copy-start(f32[128,2048]{1,0:T(8,128)} %get-tuple-element.329) | copy-start | bytes 3145732
  1548.0 43.9 %copy-start.13 = (bf16[1,128,2048]{2,1,0:T(8,128)(2,1)S(1)}, bf16[1,128,2048]{2,1,0:T(8,128)(2,1)}, u32[]{:S(2)}) copy-start(bf16[1,128,2048]{2,1,0:T(8,128)(2,1)} %param.31) | copy-start | bytes 1572868
  1688.8 4.3 copy-start.11
  2855.2 9.5 copy-start
Sparse Core Ops, SparseCore 0:
  9.8 55.2 all-gather.19
  67.0 52.5 all-gather.15
  122.0 26.3 all-gather.21
  150.1 87.4 all-gather.23
  239.9 26.4 all-gather.17
  268.1 87.4 all-gather.25
  357.5 227.5 all-gather.27
  587.0 227.5 all-gather.29
  816.5 227.5 all-gather.31
  1171.0 27.9 reduce-scatter.6
  1202.5 27.9 reduce-scatter.8
  1232.1 56.7 all-gather.41
  1290.8 35.1 all-gather.39
  1328.2 55.8 all-gather.33
  1386.4 122.3 all-gather.35
  1512.2 176.5 all-reduce.3
  1690.3 1114.8 all-gather.37
